TPU v7x, 256 devices: a whole 4x4x8 slice. The times are simulated.
256 devices in a mesh: grp: 4 (over z_lo), mem: 64 (over x, z_hi, y, core).
Axes of the slice: x: 4, y: 4, z: 8 (z_hi: 2, z_lo: 4; z = z_hi * 4 + z_lo), core: 2. Of those that a mesh axis runs over, the one named last changes fastest.
Arguments:
- embeddings: bfloat16 [262144, 4096], P(('grp', 'mem')), may hold values from -6 to 6
- local_picks: int32 [4, 512], P('grp', 'mem'), may hold values from 0 to 1023
- second_picks: int32 [4, 16], P('grp'), may hold values from 0 to 511
- final_picks: int32 [16], replicated, may hold values from 0 to 63
Outputs:
- gain_table: float32 [64, 512], P('grp', 'mem')
- final_cover: float32 [262144], P(('grp', 'mem'))
Inputs may be any that keep to these rules, and one draw needn't show every extreme that they name: `local_picks`: entry (g, m * 8 + k) names a row among the 1024 points of device m of group g; repeats may occur. `second_picks`: candidate indices of the group, in greedy order; repeats may occur. `final_picks`: index g * 16 + t names group g's second-round pick t; repeats may occur.
All inputs are finite; a program needn't handle non-finite values.
Results may differ from a plain program's by a relative error of at most 0.0003.
Values may be sent and summed in bfloat16 or wider, within the bound.
A program may use at most 64 MiB of HBM per device.

v0:
```python
import jax
import jax.numpy as jnp
from jax import lax
from jax.sharding import PartitionSpec as P

D = 4096


def split_up(x, dim, size):
    before, after = (x.shape[:dim], x.shape[dim + 1 :])
    return jnp.moveaxis(x.reshape(*before, size, -1, *after), dim, 0)


def sent_and_summed(x, axis, dim):
    parts = split_up(x, dim, lax.axis_size(axis))
    arrived = lax.all_to_all(parts, axis, split_axis=0, concat_axis=0, tiled=True)
    return arrived.sum(axis=0)


def per_device(embeddings, local_picks, second_picks, final_picks):
    scaling = float(D) ** (-0.5)
    point_count = embeddings.shape[0]
    local_count = local_picks.shape[1]
    second_list = second_picks[0]
    rounds = second_list.shape[0]
    member = lax.axis_index("mem")
    choose = (local_picks[0][:, None] == lax.iota(jnp.int32, point_count)[None, :]).astype(
        jnp.bfloat16
    )
    own_rows = jnp.dot(choose, embeddings, preferred_element_type=jnp.float32).astype(jnp.bfloat16)

    def similar(other_rows):
        dims = (((1,), (1,)), ((), ()))
        return (
            lax.dot_general(embeddings, other_rows, dims, preferred_element_type=jnp.float32)
            * scaling
        )

    similar_map = similar(lax.all_gather(own_rows, "mem", axis=0, tiled=True))
    group_index = lax.axis_index("grp")
    wanted_group = final_picks // rounds
    winner_slot = final_picks % rounds
    cand_index = jnp.take(second_list, winner_slot)
    owned = (wanted_group == group_index) & (cand_index // local_count == member)
    local_slot = cand_index - member * local_count
    select_table = (
        (local_slot[:, None] == lax.iota(jnp.int32, local_count)[None, :]) & owned[:, None]
    ).astype(jnp.bfloat16)
    row_terms = jnp.dot(select_table, own_rows, preferred_element_type=jnp.float32)
    final_rows = lax.psum(row_terms, ("grp", "mem")).astype(jnp.bfloat16)
    own_block = lax.dynamic_slice_in_dim(similar_map, member * local_count, local_count, 1)
    coverage = jnp.max(own_block, axis=1)
    chosen_cols = jnp.take(similar_map, second_list, axis=1)

    def greedy_step(cover_now, column):
        partial_value = jnp.sum(jnp.maximum(similar_map - cover_now[:, None], 0.0), axis=0)
        return (jnp.maximum(cover_now, column), partial_value)

    _, partials = lax.scan(greedy_step, coverage, chosen_cols.T)
    gain_table = sent_and_summed(partials, "mem", 1) / point_count
    final_cover = jnp.max(similar(final_rows), axis=1)
    return (gain_table, final_cover)


def solution(mesh):
    placed = (P(("grp", "mem"), None), P("grp", "mem"), P("grp", None), P())
    return jax.shard_map(
        per_device,
        mesh=mesh,
        in_specs=placed,
        out_specs=(P("grp", "mem"), P(("grp", "mem"))),
        check_vma=False,
    )
```

profile of v0, /device:TPU:1, one launch (start us, length us, event | category | flops | bytes accessed | tf_op | source)
XLA Modules:
  0.0 156.5 jit_solution(1627441644940368098)
XLA Ops:
  7.2 5.3 %convolution_convert_fusion = bf16[8,4096]{1,0:T(8,128)(2,1)} fusion(bf16[1024,4096]{1,0:T(8,128)(2,1)} %param.6, s32[8]{0:T(128)} %bitcast.33), kind=kOutput, calls=%fused_computation.4 | convolution fusion | flops 67149824 | bytes 8454176 | tf_op jit(solution)/shard_map/dot_general | solution.py:30
  12.6 0.7 gather_fusion.1
  13.3 1.1 fusion.4
  14.4 85.0 %all-reduce.1 = bf16[16,4096]{1,0:T(8,128)(2,1)S(1)} all-reduce(f32[16,4096]{1,0:T(8,128)S(1)} %fusion.4), channel_id=1, replica_groups=mesh['grp'=4,'mem'=64] {'grp','mem'}, use_global_device_ids=true, to_apply=%region_5.6 | all-reduce | flops 65536 | bytes 393216 | tf_op jit(solution)/shard_map/psum | solution.py:50
  99.5 10.2 %all-gather.2.cloned.1.call-done = bf16[512,4096]{1,0:T(8,128)(2,1)} async-done(((bf16[8,4096]{1,0:T(8,128)(2,1)}), bf16[512,4096]{1,0:T(8,128)(2,1)}) %all-gather.2.cloned.1.call-update) | async-done | bytes 4194320 | tf_op jit(solution)/shard_map/all_gather | solution.py:39
  109.7 8.2 %convolution_multiply_fusion = f32[512,1024]{1,0:T(8,128)S(1)} fusion(bf16[512,4096]{1,0:T(8,128)(2,1)} %all-gather.2.cloned.1.call-done, bf16[1024,4096]{1,0:T(8,128)(2,1)} %param.6), kind=kOutput, calls=%fused_computation.5 | convolution fusion | flops 4295491584 | bytes 14680064 | tf_op jit(solution)/shard_map/dot_general | solution.py:35
  117.9 1.3 copy-done.1
  119.2 1.9 %copy.7 = f32[1024,512]{1,0:T(8,128)S(1)} copy(f32[1024,512]{0,1:T(8,128)} %bitcast.29) | data formatting | bytes 4194304 | tf_op jit(solution)/shard_map/while | solution.py:59
  121.2 2.2 %gather_fusion = f32[16,1024]{1,0:T(8,128)S(1)} fusion(f32[1024,512]{0,1:T(8,128)} %bitcast.30, s32[1024]{0:T(1024)S(1)} %pad_clamp_fusion.1), kind=kCustom, calls=%fused_computation | custom fusion | bytes 131136 | tf_op jit(solution)/shard_map/jit(_take)/gather | solution.py:53
  123.5 6.4 %while.12 = (s32[]{:T(128)}, f32[1024]{0:T(1024)S(1)}, f32[16,512]{1,0:T(8,128)S(1)}, f32[16,1024]{1,0:T(8,128)S(1)}, f32[1024,512]{1,0:T(8,128)S(1)}, /*index=5*/s32[]{:T(128)}, s32[]{:T(128)}) while((s32[]{:T(128)}, f32[1024]{0:T(1024)S(1)}, f32[16,512]{1,0:T(8,128)S(1)}, f32[16,1024]{1,0:T(8,128)S(1)}, f32[1024,512]{1,0:T(8,128)S(1)}, ...), condition=%wide.region_3.4_spmd, body=%wide.region_1.3_spmd.sunk | while | flops 1573378 | bytes 2127965 | solution.py:59
  123.9 0.3 maximum_reduce_fusion.2
  124.3 0.3 maximum_reduce_fusion.2
  124.7 0.3 maximum_reduce_fusion.2
  125.1 0.3 maximum_reduce_fusion.2
  125.5 0.3 maximum_reduce_fusion.2
  125.9 0.3 maximum_reduce_fusion.2
  126.3 0.3 maximum_reduce_fusion.2
  126.7 0.3 maximum_reduce_fusion.2
  127.1 0.3 maximum_reduce_fusion.2
  127.5 0.3 maximum_reduce_fusion.2
  127.9 0.3 maximum_reduce_fusion.2
  128.3 0.3 maximum_reduce_fusion.2
  128.7 0.3 maximum_reduce_fusion.2
  129.1 0.3 maximum_reduce_fusion.2
  129.5 0.3 maximum_reduce_fusion.2
  130.0 0.8 reshape.71
  130.8 5.1 %all-to-all-start = ((f32[64,1,128]{2,1,0:T(1,128)}), f32[64,1,128]{2,1,0:T(1,128)S(1)}, u32[]{:S(2)}, u32[]{:S(2)}) async-start(f32[64,1,128]{2,1,0:T(1,128)} %reshape.71), calls=%async_computation | async-start | bytes 65536 | tf_op jit(solution)/shard_map/all_to_all | solution.py:16
  135.9 6.3 %fusion = f32[1024]{0:T(1024)} fusion(bf16[1024,4096]{1,0:T(8,128)(2,1)} %param.6, bf16[16,4096]{1,0:T(8,128)(2,1)S(1)} %all-reduce.1), kind=kOutput, calls=%fused_computation.7 | convolution fusion | flops 134249472 | bytes 8523776 | tf_op jit(solution)/shard_map/dot_general | solution.py:35
  142.1 5.5 %all-to-all-done = f32[64,1,128]{2,1,0:T(1,128)S(1)} async-done(((f32[64,1,128]{2,1,0:T(1,128)}), f32[64,1,128]{2,1,0:T(1,128)S(1)}, u32[]{:S(2)}, u32[]{:S(2)}) %all-to-all-start) | async-done | bytes 32800 | tf_op jit(solution)/shard_map/all_to_all | solution.py:16
  147.6 0.5 broadcast.98
  148.1 0.7 reduce.2
  149.0 0.6 broadcast_multiply_fusion
  (70 shorter events, 2.1 us)
Async XLA Ops:
  7.2 102.5 %all-gather.2.cloned.1.call-start = ((), (), s32[]{:S(2)}) async-start(), calls=%async_computation.1 | async-start | bytes 4259840 | tf_op jit(solution)/shard_map/all_gather | solution.py:39
  7.2 5.3 %copy-start.2 = (s32[16]{0:T(128)S(1)}, s32[16]{0:T(128)}, u32[]{:S(2)}) copy-start(s32[16]{0:T(128)} %param.9) | copy-start | bytes 196
  7.2 5.4 %copy-start = (s32[1,16]{1,0:T(1,128)S(1)}, s32[1,16]{1,0:T(1,128)}, u32[]{:S(2)}) copy-start(s32[1,16]{1,0:T(1,128)} %param.8) | copy-start | bytes 196
  117.9 1.4 copy-start.1
  130.8 16.8 %all-to-all-start = ((f32[64,1,128]{2,1,0:T(1,128)}), f32[64,1,128]{2,1,0:T(1,128)S(1)}, u32[]{:S(2)}, u32[]{:S(2)}) async-start(f32[64,1,128]{2,1,0:T(1,128)} %reshape.71), calls=%async_computation | async-start | bytes 65536 | tf_op jit(solution)/shard_map/all_to_all | solution.py:16
Sparse Core Ops, SparseCore 0:
  12.7 96.9 all-gather.1
where the time goes:
time: 157 us; the launch traced here: 156 us
  blocking collectives  85 us (54%)
  matrix products  20.8 us (13%)
  waiting for transfers between devices  15.7 us (10%)
  between operations  14.2 us (9%)
  local copies, waits for them, and re-layouts  8.8 us (6%)
  other arithmetic  6.21 us (4%)
  starting transfers between devices  5.12 us (3%)
    psum x1, blocking collectives, per_device(): final_rows = lax.psum(row_terms, ('grp', 'mem')).astype(jnp.bfloat16)  85 us
    dot_general x2, matrix products, similar(): lax.dot_general(embeddings, other_rows, dims, preferred_element_type=jnp....  14.5 us
    all_gather x1, waiting for transfers between devices, per_device(): similar_map = similar(lax.all_gather(own_rows, 'mem', axis=0, tiled=True))  10.2 us
    all_to_all x1, waiting for transfers between devices, sent_and_summed(): lax.all_to_all(parts, axis, split_axis=0, concat_axis=0, tiled=True)  5.46 us
    dot_general x1, matrix products, per_device(): jnp.dot(choose, embeddings, preferred_element_type=jnp.float32)  5.28 us
    all_to_all x1, starting transfers between devices, sent_and_summed(): lax.all_to_all(parts, axis, split_axis=0, concat_axis=0, tiled=True)  5.08 us
    reduce_sum x16, other arithmetic, greedy_step(): jnp.sum(jnp.maximum(similar_map - cover_now[:, None], 0.0), axis=0)  4.57 us
  transfers between devices with their start and end apart: 2, of which 2 were waited for; matrix products, arithmetic and copies ran while one was open for 5% of the time, Pallas kernels for 0%

commit v1 on v0

--- a/solution.py
+++ b/solution.py
@@ -4,6 +4,13 @@
 from jax.sharding import PartitionSpec as P
 
 D = 4096
+
+
+def swapped_in(x, axis, d):
+    size = lax.axis_size(axis)
+    blocks = jnp.stack([x for _ in range(size)])
+    blocks = lax.all_to_all(blocks, axis, split_axis=0, concat_axis=0)
+    return jnp.concatenate(blocks, axis=d)
 
 
 def split_up(x, dim, size):
@@ -36,7 +43,7 @@
             * scaling
         )
 
-    similar_map = similar(lax.all_gather(own_rows, "mem", axis=0, tiled=True))
+    similar_map = similar(swapped_in(own_rows, "mem", 0))
     group_index = lax.axis_index("grp")
     wanted_group = final_picks // rounds
     winner_slot = final_picks % rounds

time: 157 us -> 206 us (1.31)
  blocking collectives: 85 us -> 139 us
  starting transfers between devices: 5.12 us -> 23.3 us
  between operations: 14.2 us -> 0.83 us
  waiting for transfers between devices: 15.7 us -> 5.46 us
  local copies, waits for them, and re-layouts: 8.8 us -> 11.3 us
    psum x1, blocking collectives: 85 us -> 139 us  [per_device(): final_rows = lax.psum(row_terms, ('grp', 'mem')).astype(jnp.bfloat16)]
    all_to_all x0 -> x1, starting transfers between devices: none -> 15.9 us  [swapped_in(): blocks = lax.all_to_all(blocks, axis, split_axis=0, concat_axis=0)]
    all_gather x1 -> x0, waiting for transfers between devices: 10.2 us -> none  [per_device(): similar_map = similar(lax.all_gather(own_rows, 'mem', axis=0, tiled=True))]
    another operation x0 -> x1, local copies, waits for them, and re-layouts: none -> 2.48 us  [swapped_in(): blocks = jnp.stack([x for _ in range(size)])]
    all_to_all x1, starting transfers between devices: 5.08 us -> 7.33 us  [sent_and_summed(): lax.all_to_all(parts, axis, split_axis=0, concat_axis=0, tiled=True)]
  transfers between devices with their start and end apart: 2 -> 2, of which waited for: 2 -> 1; matrix products, arithmetic and copies ran while one was open for 5% -> 4% of each run, Pallas kernels for 0% -> 0%
where the time goes in v1:
time: 206 us
  blocking collectives  139 us (67%)
  starting transfers between devices  23.3 us (11%)
  matrix products  19.4 us (9%)
  local copies, waits for them, and re-layouts  11.3 us (5%)
  other arithmetic  6.2 us (3%)
  waiting for transfers between devices  5.46 us (3%)
    psum x1, blocking collectives, per_device(): final_rows = lax.psum(row_terms, ('grp', 'mem')).astype(jnp.bfloat16)  139 us
    all_to_all x1, starting transfers between devices, swapped_in(): blocks = lax.all_to_all(blocks, axis, split_axis=0, concat_axis=0)  15.9 us
    dot_general x2, matrix products, similar(): lax.dot_general(embeddings, other_rows, dims, preferred_element_type=jnp....  14.5 us
    all_to_all x1, starting transfers between devices, sent_and_summed(): lax.all_to_all(parts, axis, split_axis=0, concat_axis=0, tiled=True)  7.33 us
    all_to_all x1, waiting for transfers between devices, sent_and_summed(): lax.all_to_all(parts, axis, split_axis=0, concat_axis=0, tiled=True)  5.46 us
    dot_general x1, matrix products, per_device(): jnp.dot(choose, embeddings, preferred_element_type=jnp.float32)  4.63 us
    reduce_sum x16, other arithmetic, greedy_step(): jnp.sum(jnp.maximum(similar_map - cover_now[:, None], 0.0), axis=0)  4.55 us
  transfers between devices with their start and end apart: 2, of which 1 were waited for; matrix products, arithmetic and copies ran while one was open for 4% of the time, Pallas kernels for 0%

profile of v1, /device:TPU:1, one launch (start us, length us, event | category | flops | bytes accessed | tf_op | source)
XLA Modules:
  0.0 205.9 jit_solution(7602057694090181483)
XLA Ops:
  0.6 4.6 %convolution_convert_fusion = bf16[8,4096]{1,0:T(8,128)(2,1)S(1)} fusion(bf16[1024,4096]{1,0:T(8,128)(2,1)} %param.6, s32[8]{0:T(128)} %bitcast.37), kind=kOutput, calls=%fused_computation.4 | convolution fusion | flops 67149824 | bytes 8454176 | tf_op jit(solution)/shard_map/dot_general | solution.py:37
  5.3 2.5 %stack.2 = bf16[64,8,4096]{2,1,0:T(8,128)(2,1)} broadcast(bf16[8,4096]{1,0:T(8,128)(2,1)S(1)} %convolution_convert_fusion), dimensions={1,2} | broadcast | bytes 4259840 | tf_op jit(solution)/shard_map/stack | solution.py:11
  7.7 15.9 %all-to-all-start = ((bf16[64,8,4096]{2,1,0:T(8,128)(2,1)}), bf16[64,8,4096]{2,1,0:T(8,128)(2,1)}, u32[]{:S(2)}, u32[]{:S(2)}) async-start(bf16[64,8,4096]{2,1,0:T(8,128)(2,1)} %stack.2), calls=%async_computation | async-start | bytes 8388608 | tf_op jit(solution)/shard_map/all_to_all | solution.py:12
  23.7 0.7 gather_fusion.1
  24.7 138.9 %all-reduce.1 = bf16[16,4096]{1,0:T(8,128)(2,1)S(1)} all-reduce(f32[16,4096]{1,0:T(8,128)S(1)} %fusion.9), channel_id=1, replica_groups=mesh['grp'=4,'mem'=64] {'grp','mem'}, use_global_device_ids=true, to_apply=%region_5.6 | all-reduce | flops 65536 | bytes 393216 | tf_op jit(solution)/shard_map/psum | solution.py:57
  163.6 8.2 %fusion.2 = f32[512,1024]{1,0:T(8,128)S(1)} fusion(bf16[1024,4096]{1,0:T(8,128)(2,1)} %param.6, bf16[64,8,4096]{2,1,0:T(8,128)(2,1)} %all-to-all-done), kind=kOutput, calls=%fused_computation.7 | convolution fusion | flops 4295491584 | bytes 14680064 | tf_op jit(solution)/shard_map/dot_general | solution.py:42
  171.9 1.3 copy-done.1
  173.2 1.9 copy.7
  175.2 2.2 %gather_fusion = f32[16,1024]{1,0:T(8,128)S(1)} fusion(f32[1024,512]{0,1:T(8,128)} %bitcast.34, s32[1024]{0:T(1024)S(1)} %pad_clamp_fusion.1), kind=kCustom, calls=%fused_computation | custom fusion | bytes 131136 | tf_op jit(solution)/shard_map/jit(_take)/gather | solution.py:60
  177.5 6.4 %while.12 = (s32[]{:T(128)}, f32[1024]{0:T(1024)S(1)}, f32[16,512]{1,0:T(8,128)S(1)}, f32[16,1024]{1,0:T(8,128)S(1)}, f32[1024,512]{1,0:T(8,128)S(1)}, /*index=5*/s32[]{:T(128)}, s32[]{:T(128)}) while((s32[]{:T(128)}, f32[1024]{0:T(1024)S(1)}, f32[16,512]{1,0:T(8,128)S(1)}, f32[16,1024]{1,0:T(8,128)S(1)}, f32[1024,512]{1,0:T(8,128)S(1)}, ...), condition=%wide.region_3.4_spmd, body=%wide.region_1.3_spmd.sunk | while | flops 1573378 | bytes 2127965 | solution.py:66
  177.9 0.3 maximum_reduce_fusion.2
  178.3 0.3 maximum_reduce_fusion.2
  178.7 0.3 maximum_reduce_fusion.2
  179.1 0.3 maximum_reduce_fusion.2
  179.5 0.3 maximum_reduce_fusion.2
  179.9 0.3 maximum_reduce_fusion.2
  180.3 0.3 maximum_reduce_fusion.2
  180.7 0.3 maximum_reduce_fusion.2
  181.1 0.3 maximum_reduce_fusion.2
  181.5 0.3 maximum_reduce_fusion.2
  181.9 0.3 maximum_reduce_fusion.2
  182.3 0.3 maximum_reduce_fusion.2
  182.7 0.3 maximum_reduce_fusion.2
  183.1 0.3 maximum_reduce_fusion.2
  183.5 0.3 maximum_reduce_fusion.2
  184.0 0.8 reshape.77
  184.8 7.3 %all-to-all-start.1 = ((f32[64,1,128]{2,1,0:T(1,128)}), f32[64,1,128]{2,1,0:T(1,128)S(1)}, u32[]{:S(2)}, u32[]{:S(2)}) async-start(f32[64,1,128]{2,1,0:T(1,128)} %reshape.77), calls=%async_computation.1 | async-start | bytes 65536 | tf_op jit(solution)/shard_map/all_to_all | solution.py:23
  192.1 6.3 %fusion.5 = f32[1024]{0:T(1024)} fusion(bf16[1024,4096]{1,0:T(8,128)(2,1)} %param.6, bf16[16,4096]{1,0:T(8,128)(2,1)S(1)} %all-reduce.1), kind=kOutput, calls=%fused_computation.9 | convolution fusion | flops 134249472 | bytes 8523776 | tf_op jit(solution)/shard_map/dot_general | solution.py:42
  198.4 5.5 %all-to-all-done.1 = f32[64,1,128]{2,1,0:T(1,128)S(1)} async-done(((f32[64,1,128]{2,1,0:T(1,128)}), f32[64,1,128]{2,1,0:T(1,128)S(1)}, u32[]{:S(2)}, u32[]{:S(2)}) %all-to-all-start.1) | async-done | bytes 32800 | tf_op jit(solution)/shard_map/all_to_all | solution.py:23
  203.8 0.5 broadcast.100
  204.3 0.7 reduce.2
  205.3 0.6 broadcast_multiply_fusion
  (70 shorter events, 2.3 us)
Async XLA Ops:
  7.7 16.0 %copy-start.2 = (s32[16]{0:T(128)S(1)}, s32[16]{0:T(128)}, u32[]{:S(2)}) copy-start(s32[16]{0:T(128)} %param.9) | copy-start | bytes 196
  7.7 16.0 %copy-start = (s32[1,16]{1,0:T(1,128)S(1)}, s32[1,16]{1,0:T(1,128)}, u32[]{:S(2)}) copy-start(s32[1,16]{1,0:T(1,128)} %param.8) | copy-start | bytes 196
  7.7 155.9 %all-to-all-start = ((bf16[64,8,4096]{2,1,0:T(8,128)(2,1)}), bf16[64,8,4096]{2,1,0:T(8,128)(2,1)}, u32[]{:S(2)}, u32[]{:S(2)}) async-start(bf16[64,8,4096]{2,1,0:T(8,128)(2,1)} %stack.2), calls=%async_computation | async-start | bytes 8388608 | tf_op jit(solution)/shard_map/all_to_all | solution.py:12
  171.9 1.4 copy-start.1
  184.8 19.1 %all-to-all-start.1 = ((f32[64,1,128]{2,1,0:T(1,128)}), f32[64,1,128]{2,1,0:T(1,128)S(1)}, u32[]{:S(2)}, u32[]{:S(2)}) async-start(f32[64,1,128]{2,1,0:T(1,128)} %reshape.77), calls=%async_computation.1 | async-start | bytes 65536 | tf_op jit(solution)/shard_map/all_to_all | solution.py:23
